TPU v7x, 32 devices: a whole 2x2x4 slice. The times are simulated.
32 devices in a mesh: zero: 2 (over core), tp: 4 (over y, x), job: 4 (over z).
Axes of the slice: x: 2, y: 2, z: 4, core: 2. Of those that a mesh axis runs over, the one named last changes fastest.
Arguments:
- w_query: float32 [16384, 4096], P(('job', 'zero'), 'tp'), parts along dimension 0, may hold values from -0.125 to 0.125
- avg_query: float32 [16384, 4096], P(('job', 'zero'), 'tp'), parts along dimension 0, may hold values from -0.09375 to 0.09375
- w_key: float32 [16384, 1024], P(('job', 'zero'), 'tp'), parts along dimension 0, may hold values from -0.125 to 0.125
- avg_key: float32 [16384, 1024], P(('job', 'zero'), 'tp'), parts along dimension 0, may hold values from -0.09375 to 0.09375
- w_value: float32 [16384, 1024], P(('job', 'zero'), 'tp'), parts along dimension 0, may hold values from -0.125 to 0.125
- avg_value: float32 [16384, 1024], P(('job', 'zero'), 'tp'), parts along dimension 0, may hold values from -0.09375 to 0.09375
- norm_train: float32 [16384], P(('job', 'zero', 'tp')), parts along dimension 0, may hold values from 0.25 to 1.75
- norm_step: float32 [16384], P(('job', 'zero', 'tp')), parts along dimension 0, may hold values from -0.3 to 0.3
Outputs:
- serve_query: bfloat16 [16384, 4096], P('job', 'tp'), parts along dimension 0
- serve_key: bfloat16 [16384, 1024], P('job', 'tp'), parts along dimension 0
- serve_value: bfloat16 [16384, 1024], P('job', 'tp'), parts along dimension 0
- column_query: float32 [16384], P(('job', 'tp')), parts along dimension 0
- column_key: float32 [4096], P(('job', 'tp')), parts along dimension 0
- column_value: float32 [4096], P(('job', 'tp')), parts along dimension 0
- serve_norm: bfloat16 [16384], P('job'), parts along dimension 0
- fresh_query: float32 [16384, 4096], P(('job', 'zero'), 'tp'), parts along dimension 0
- fresh_key: float32 [16384, 1024], P(('job', 'zero'), 'tp'), parts along dimension 0
- fresh_value: float32 [16384, 1024], P(('job', 'zero'), 'tp'), parts along dimension 0
There are 4 independent parts, one for each index of `job`. A program takes and returns all parts, laid end to end along the dimension named above; each array names one. Nothing has to cross between parts.
All inputs are finite; a program needn't handle non-finite values.
Results may differ from a plain program's by a relative error of at most 0.001.
Values may be sent and summed in bfloat16 or wider, within the bound.
A program may use at most 128 MiB of HBM per device.

v0:
```python
import jax
import jax.numpy as jnp
from jax import lax
from jax.sharding import PartitionSpec as P

keep_rate = 0.75


def body(w_query, avg_query, w_key, avg_key, w_value, avg_value, norm_train, norm_step):
    fresh_query = keep_rate * avg_query + (1.0 - keep_rate) * w_query
    fresh_key = keep_rate * avg_key + (1.0 - keep_rate) * w_key
    fresh_value = keep_rate * avg_value + (1.0 - keep_rate) * w_value
    total_query, total_key, total_value = lax.psum(
        (
            jnp.sum(fresh_query * fresh_query, axis=0),
            jnp.sum(fresh_key * fresh_key, axis=0),
            jnp.sum(fresh_value * fresh_value, axis=0),
        ),
        "zero",
    )
    column_query = jnp.sqrt(total_query)
    column_key = jnp.sqrt(total_key)
    column_value = jnp.sqrt(total_value)
    narrow_query, narrow_key, narrow_value = (
        (fresh_query / column_query).astype(jnp.bfloat16),
        (fresh_key / column_key).astype(jnp.bfloat16),
        (fresh_value / column_value).astype(jnp.bfloat16),
    )
    serve_query, serve_key, serve_value = (
        lax.all_gather(narrow_query, "zero", axis=0, tiled=True),
        lax.all_gather(narrow_key, "zero", axis=0, tiled=True),
        lax.all_gather(narrow_value, "zero", axis=0, tiled=True),
    )
    serve_norm = lax.all_gather(
        (norm_train + norm_step).astype(jnp.bfloat16), ("zero", "tp"), axis=0, tiled=True
    )
    return (
        serve_query,
        serve_key,
        serve_value,
        column_query,
        column_key,
        column_value,
        serve_norm,
        fresh_query,
        fresh_key,
        fresh_value,
    )


def solution(mesh):
    in_specs = (
        P(("job", "zero"), "tp"),
        P(("job", "zero"), "tp"),
        P(("job", "zero"), "tp"),
        P(("job", "zero"), "tp"),
        P(("job", "zero"), "tp"),
        P(("job", "zero"), "tp"),
        P(("job", "zero", "tp")),
        P(("job", "zero", "tp")),
    )
    out_specs = (
        P("job", "tp"),
        P("job", "tp"),
        P("job", "tp"),
        P(("job", "tp")),
        P(("job", "tp")),
        P(("job", "tp")),
        P("job"),
        P(("job", "zero"), "tp"),
        P(("job", "zero"), "tp"),
        P(("job", "zero"), "tp"),
    )
    return jax.shard_map(body, mesh=mesh, in_specs=in_specs, out_specs=out_specs, check_vma=False)
```

profile of v0, /device:TPU:0, one launch (start us, length us, event | category | flops | bytes accessed | tf_op | source)
XLA Modules:
  0.0 94.4 jit_solution(11857054068180849463)
XLA Ops:
  7.2 0.0 all-gather.7.cloned.1.call-start
  7.2 0.0 copy-start.3
  7.2 0.0 copy-start.4
  7.2 0.0 copy-start.5
  7.3 0.0 copy-start.6
  7.3 10.0 %multiply_reduce_fusion = (f32[1024]{0:T(1024)S(1)}, f32[2048,1024]{1,0:T(8,128)}) fusion(f32[2048,1024]{1,0:T(8,128)} %param.8, f32[2048,1024]{1,0:T(8,128)} %param.9), kind=kLoop, calls=%fused_computation.1 | loop fusion | flops 10484736 | bytes 25169920 | tf_op jit(solution)/shard_map/reduce_sum | solution.py:15
  17.3 0.0 copy-done.3
  17.3 0.0 copy-done.4
  17.3 0.0 copy-done.5
  17.3 1.3 %copy-done.6 = f32[2048,256]{1,0:T(8,128)S(1)} copy-done((f32[2048,256]{1,0:T(8,128)S(1)}, f32[2048,256]{1,0:T(8,128)}, u32[]{:S(2)}) %copy-start.6) | copy-done | bytes 2097176
  18.6 2.0 %multiply_reduce_fusion.1 = (f32[256]{0:T(256)S(1)}, f32[2048,256]{1,0:T(8,128)S(1)}, f32[256]{0:T(256)S(1)}, f32[2048,256]{1,0:T(8,128)}) fusion(f32[2048,256]{1,0:T(8,128)S(1)} %copy-done.3, f32[2048,256]{1,0:T(8,128)S(1)} %copy-done.4, f32[2048,256]{1,0:T(8,128)S(1)} %copy-done.5, f32[2048,256]{1,0:T(8,128)S(1)} %copy-done.6), kind=kLoop, calls=%fused_computation.4 | loop fusion | flops 5242368 | bytes 12584960 | tf_op jit(solution)/shard_map/reduce_sum | solution.py:17
  20.6 0.0 copy-start
  20.6 2.6 %all-reduce = (f32[1024]{0:T(1024)S(1)}, f32[256]{0:T(256)S(1)}, f32[256]{0:T(256)S(1)}) all-reduce(f32[1024]{0:T(1024)S(1)} %get-tuple-element.17, f32[256]{0:T(256)S(1)} %get-tuple-element.19, f32[256]{0:T(256)S(1)} %get-tuple-element.13), channel_id=1, replica_groups=mesh['zero'=2,'tp'=4,'job'=4] {'zero'}, use_global_device_ids=true, to_apply=%region_1.0 | all-reduce | flops 1536 | bytes 12288 | tf_op jit(solution)/shard_map/psum | solution.py:13
  23.2 0.0 copy-start.8
  23.2 2.7 %divide_convert_fusion.2 = bf16[2048,256]{1,0:T(8,128)(2,1)} fusion(f32[2048,256]{1,0:T(8,128)} %get-tuple-element.39, f32[256]{0:T(256)S(1)} %sqrt.10), kind=kLoop, calls=%fused_computation.6 | loop fusion | flops 1048576 | bytes 3146752 | tf_op jit(solution)/shard_map/convert_element_type | solution.py:26
  25.9 0.0 all-gather.7.cloned.1.call-update
  26.0 0.0 copy-done.8
  26.0 0.0 all-gather.9.cloned.1.call-start
  26.0 0.0 copy-start.9
  26.0 0.0 copy-done
  26.1 1.1 %divide_convert_fusion.1 = bf16[2048,256]{1,0:T(8,128)(2,1)} fusion(f32[2048,256]{1,0:T(8,128)S(1)} %get-tuple-element.40, f32[256]{0:T(256)S(1)} %sqrt.11), kind=kLoop, calls=%fused_computation.3 | loop fusion | flops 1048576 | bytes 3146752 | tf_op jit(solution)/shard_map/convert_element_type | solution.py:27
  27.2 0.0 all-gather.9.cloned.1.call-update
  27.2 0.0 copy-done.9
  27.2 0.0 all-gather.5.cloned.1.call-start
  27.3 0.0 copy-start.7
  27.3 6.7 %divide_convert_fusion = bf16[2048,1024]{1,0:T(8,128)(2,1)} fusion(f32[2048,1024]{1,0:T(8,128)} %get-tuple-element.38, f32[1024]{0:T(1024)S(1)} %sqrt.9), kind=kLoop, calls=%fused_computation | loop fusion | flops 4194304 | bytes 12587008 | tf_op jit(solution)/shard_map/convert_element_type | solution.py:25
  34.0 0.0 copy-done.7
  34.0 0.0 copy-start.10
  34.0 0.0 copy-start.11
  34.0 0.0 all-gather.5.cloned.1.call-update
  34.0 0.7 copy-done.10
  34.7 0.0 copy-done.11
  34.7 20.4 %all-gather = bf16[8,1,512]{2,1,0:T(2,128)(2,1)S(1)} all-gather(bf16[1,1,512]{2,1,0:T(2,128)(2,1)S(1)} %reshape.23), channel_id=1, replica_groups=mesh['zero'=2,'tp'=4,'job'=4] {'zero','tp'}, dimensions={0}, use_global_device_ids=true | all-gather | bytes 9216 | tf_op jit(solution)/shard_map/all_gather | solution.py:34
  55.2 0.6 copy.18
  55.8 0.0 all-gather.7.cloned.1.call-done
  55.8 0.0 all-gather.9.cloned.1.call-done
  55.8 20.5 %all-gather.5.cloned.1.call-done = bf16[4096,1024]{1,0:T(8,128)(2,1)} async-done(((bf16[2048,1024]{1,0:T(8,128)(2,1)}), bf16[4096,1024]{1,0:T(8,128)(2,1)}) %all-gather.5.cloned.1.call-update) | async-done | bytes 8388624 | tf_op jit(solution)/shard_map/all_gather | solution.py:30
  76.3 0.0 copy-start.1
  76.3 7.9 %copy.22 = bf16[4096,1024]{1,0:T(8,128)(2,1)} copy(bf16[4096,1024]{1,0:T(8,128)(2,1)} %all-gather.5.cloned.1.call-done) | data formatting | bytes 16777216
  84.2 0.0 copy-done.1
  84.2 0.0 copy-start.2
  84.2 1.3 %copy.23 = bf16[4096,256]{1,0:T(8,128)(2,1)} copy(bf16[4096,256]{1,0:T(8,128)(2,1)S(1)} %copy-done.1) | data formatting | bytes 4194304
  85.6 1.0 %copy-done.2 = bf16[4096,256]{1,0:T(8,128)(2,1)S(1)} copy-done((bf16[4096,256]{1,0:T(8,128)(2,1)S(1)}, bf16[4096,256]{1,0:T(8,128)(2,1)}, u32[]{:S(2)}) %copy-start.2) | copy-done | bytes 2097176
  86.6 1.3 %copy.24 = bf16[4096,256]{1,0:T(8,128)(2,1)} copy(bf16[4096,256]{1,0:T(8,128)(2,1)S(1)} %copy-done.2) | data formatting | bytes 4194304
  (6 shorter events, 0.1 us)
Async XLA Ops:
  7.2 48.6 %all-gather.7.cloned.1.call-start = ((), (), s32[]{:S(2)}) async-start(), calls=%async_computation.1 | async-start | bytes 3145728 | tf_op jit(solution)/shard_map/all_gather | solution.py:31
  7.2 10.0 %copy-start.3 = (f32[2048,256]{1,0:T(8,128)S(1)}, f32[2048,256]{1,0:T(8,128)}, u32[]{:S(2)}) copy-start(f32[2048,256]{1,0:T(8,128)} %param.12) | copy-start | bytes 6291460
  7.2 10.0 %copy-start.4 = (f32[2048,256]{1,0:T(8,128)S(1)}, f32[2048,256]{1,0:T(8,128)}, u32[]{:S(2)}) copy-start(f32[2048,256]{1,0:T(8,128)} %param.13) | copy-start | bytes 6291460
  7.2 10.0 %copy-start.5 = (f32[2048,256]{1,0:T(8,128)S(1)}, f32[2048,256]{1,0:T(8,128)}, u32[]{:S(2)}) copy-start(f32[2048,256]{1,0:T(8,128)} %param.10) | copy-start | bytes 6291460
  7.3 11.3 %copy-start.6 = (f32[2048,256]{1,0:T(8,128)S(1)}, f32[2048,256]{1,0:T(8,128)}, u32[]{:S(2)}) copy-start(f32[2048,256]{1,0:T(8,128)} %param.11) | copy-start | bytes 6291460
  20.6 5.5 %copy-start = (f32[2048,256]{1,0:T(8,128)}, f32[2048,256]{1,0:T(8,128)S(1)}, u32[]{:S(2)}) copy-start(f32[2048,256]{1,0:T(8,128)S(1)} %get-tuple-element.40) | copy-start | bytes 6291460
  23.2 2.8 %copy-start.8 = (f32[256]{0:T(256)}, f32[256]{0:T(256)S(1)}, u32[]{:S(2)}) copy-start(f32[256]{0:T(256)S(1)} %sqrt.10) | copy-start | bytes 3076
  26.0 29.8 %all-gather.9.cloned.1.call-start = ((), (), s32[]{:S(2)}) async-start(), calls=%async_computation.2 | async-start | bytes 3145728 | tf_op jit(solution)/shard_map/all_gather | solution.py:32
  26.0 1.2 %copy-start.9 = (f32[256]{0:T(256)}, f32[256]{0:T(256)S(1)}, u32[]{:S(2)}) copy-start(f32[256]{0:T(256)S(1)} %sqrt.11) | copy-start | bytes 3076
  27.2 49.1 %all-gather.5.cloned.1.call-start = ((), (), s32[]{:S(2)}) async-start(), calls=%async_computation | async-start | bytes 12582912 | tf_op jit(solution)/shard_map/all_gather | solution.py:30
  27.3 6.7 %copy-start.7 = (f32[1024]{0:T(1024)}, f32[1024]{0:T(1024)S(1)}, u32[]{:S(2)}) copy-start(f32[1024]{0:T(1024)S(1)} %sqrt.9) | copy-start | bytes 12292
  34.0 0.7 copy-start.10
  34.0 0.7 copy-start.11
  76.3 7.9 %copy-start.1 = (bf16[4096,256]{1,0:T(8,128)(2,1)S(1)}, bf16[4096,256]{1,0:T(8,128)(2,1)}, u32[]{:S(2)}) copy-start(bf16[4096,256]{1,0:T(8,128)(2,1)} %all-gather.7.cloned.1.call-done) | copy-start | bytes 6291460
  84.2 2.3 %copy-start.2 = (bf16[4096,256]{1,0:T(8,128)(2,1)S(1)}, bf16[4096,256]{1,0:T(8,128)(2,1)}, u32[]{:S(2)}) copy-start(bf16[4096,256]{1,0:T(8,128)(2,1)} %all-gather.9.cloned.1.call-done) | copy-start | bytes 6291460
Sparse Core Ops, SparseCore 0:
  26.1 13.1 all-gather.6
  41.4 11.7 all-gather.8
  55.3 21.0 all-gather.4
where the time goes:
time: 94.7 us; the launch traced here: 94.4 us
  blocking collectives  23.1 us (24%)
  other arithmetic  22.6 us (24%)
  waiting for transfers between devices  20.6 us (22%)
  local copies, waits for them, and re-layouts  14.2 us (15%)
  between operations  13.9 us (15%)
    all_gather x1, waiting for transfers between devices, body(): lax.all_gather(narrow_query, 'zero', axis=0, tiled=True)  20.5 us
    all_gather x1, blocking collectives, body(): lax.all_gather((norm_train + norm_step).astype(jnp.bfloat16), ('zero', 't...  20.4 us
    unnamed x29, local copies, waits for them, and re-layouts  14.2 us
    reduce_sum x1, other arithmetic, body(): jnp.sum(fresh_query * fresh_query, axis=0)  9.99 us
    convert_element_type x1, other arithmetic, body(): (fresh_query / column_query).astype(jnp.bfloat16)  6.67 us
    convert_element_type x1, other arithmetic, body(): (fresh_key / column_key).astype(jnp.bfloat16)  2.73 us
    psum x1, blocking collectives, body(): lax.psum((jnp.sum(fresh_query * fresh_query, axis=0), jnp.sum(fresh_key *...  2.63 us
    reduce_sum x1, other arithmetic, body(): jnp.sum(fresh_value * fresh_value, axis=0)  2 us
  transfers between devices with their start and end apart: 3, of which 1 were waited for; matrix products, arithmetic and copies ran while one was open for 9% of the time, Pallas kernels for 0%

commit v1 on v0

v1 whole, which is shorter than its diff:
```python
import functools
import math

import jax
import jax.numpy as jnp
from jax import lax
from jax.experimental import pallas as pl
from jax.experimental.pallas import tpu as pltpu
from jax.sharding import PartitionSpec as P

keep_rate = 0.75
LANES = 128
CHUNK = 256
AHEAD = 3
LAG = 1
STEP = 64
MESH = pl.DeviceIdType.MESH


def row_step(rows):
    return math.gcd(rows, STEP)


def exchange(zero, tp, counts, width, *refs):
    (wq, aq, wk, ak, wv, av, train, step, fresh, serve, scales, gain,
     w_buf, a_buf, parts, read_sem, part_send, part_recv, send, recv, gain_send, gain_recv) = refs
    chunks = sum(counts)
    rows = wq.shape[0]
    me = lax.axis_index("zero")
    my_tp = lax.axis_index("tp")
    where = []
    for w, a, count in ((wq, aq, counts[0]), (wk, ak, counts[1]), (wv, av, counts[2])):
        where += [(w, a, j * width) for j in range(count)]

    def reads(c):
        w, a, at = where[c]
        return (
            pltpu.make_async_copy(w.at[:, pl.ds(at, width)], w_buf.at[c], read_sem.at[0, c]),
            pltpu.make_async_copy(a.at[:, pl.ds(at, width)], a_buf.at[c], read_sem.at[1, c]),
        )

    for c in range(min(AHEAD, chunks)):
        for copy in reads(c):
            copy.start()

    group = zero * tp
    mine = me * tp + my_tp

    def member(d):
        other = lax.rem(mine + d, group)
        return other, {"zero": other // tp, "tp": lax.rem(other, tp)}

    barrier = pltpu.get_barrier_semaphore()
    for d in range(1, group):
        pl.semaphore_signal(barrier, inc=1, device_id=member(d)[1], device_id_type=MESH)
    pl.semaphore_wait(barrier, group - 1)

    gain[mine] = train[...] + step[...]

    def part_copy(c, d):
        return pltpu.make_async_remote_copy(
            src_ref=parts.at[me, c], dst_ref=parts.at[me, c],
            send_sem=part_send.at[c, d - 1], recv_sem=part_recv.at[c, me],
            device_id={"zero": lax.rem(me + d, zero)}, device_id_type=MESH,
        )

    def part_arrival(c, d):
        other = lax.rem(me + d, zero)
        return pltpu.make_async_remote_copy(
            src_ref=parts.at[other, c], dst_ref=parts.at[other, c],
            send_sem=part_send.at[c, d - 1], recv_sem=part_recv.at[c, other],
            device_id={"zero": other}, device_id_type=MESH,
        )

    def block(c, owner):
        return serve.at[c, pl.ds(pl.multiple_of(owner * rows, rows), rows), :]

    def serve_copy(c, d):
        return pltpu.make_async_remote_copy(
            src_ref=block(c, me), dst_ref=block(c, me),
            send_sem=send.at[c, d - 1], recv_sem=recv.at[c, me],
            device_id={"zero": lax.rem(me + d, zero)}, device_id_type=MESH,
        )

    def serve_arrival(c, d):
        other = lax.rem(me + d, zero)
        return pltpu.make_async_remote_copy(
            src_ref=block(c, other), dst_ref=block(c, other),
            send_sem=send.at[c, d - 1], recv_sem=recv.at[c, other],
            device_id={"zero": other}, device_id_type=MESH,
        )

    def gain_copy(d):
        return pltpu.make_async_remote_copy(
            src_ref=gain.at[mine], dst_ref=gain.at[mine],
            send_sem=gain_send.at[d - 1], recv_sem=gain_recv.at[mine],
            device_id=member(d)[1], device_id_type=MESH,
        )

    def gain_arrival(d):
        other, place = member(d)
        return pltpu.make_async_remote_copy(
            src_ref=gain.at[other], dst_ref=gain.at[other],
            send_sem=gain_send.at[d - 1], recv_sem=gain_recv.at[other],
            device_id=place, device_id_type=MESH,
        )

    block_rows = row_step(rows)

    def mix(c):
        if c + AHEAD < chunks:
            for copy in reads(c + AHEAD):
                copy.start()
        for copy in reads(c):
            copy.wait()

        def one(i, total):
            at = pl.ds(pl.multiple_of(i * block_rows, block_rows), block_rows)
            new = keep_rate * a_buf[c, at, :] + (1.0 - keep_rate) * w_buf[c, at, :]
            fresh[c, at, :] = new
            return total + jnp.sum((new * new).reshape(block_rows // 8, 8, width), axis=0)

        total = lax.fori_loop(0, rows // block_rows, one, jnp.zeros((8, width), jnp.float32))
        parts[me, c] = jnp.sum(total, axis=0, keepdims=True)
        for d in range(1, zero):
            part_copy(c, d).start()

    def scale(c):
        for d in range(1, zero):
            part_arrival(c, d).wait_recv()
        total = parts[0, c]
        for k in range(1, zero):
            total = total + parts[k, c]
        column = jnp.sqrt(total)
        scales[c] = column
        inverse = jnp.broadcast_to(1.0 / column, (block_rows, width))

        def one(i, carry):
            at = pl.ds(pl.multiple_of(i * block_rows, block_rows), block_rows)
            to = pl.ds(pl.multiple_of(me * rows + i * block_rows, block_rows), block_rows)
            serve[c, to, :] = (fresh[c, at, :] * inverse).astype(jnp.bfloat16)
            return carry

        lax.fori_loop(0, rows // block_rows, one, 0)
        for d in range(1, zero):
            serve_copy(c, d).start()

    for c in range(chunks + LAG):
        if c < chunks:
            mix(c)
        if c == 0:
            for d in range(1, group):
                gain_copy(d).start()
        if c >= LAG:
            scale(c - LAG)

    for d in range(1, group):
        gain_copy(d).wait_send()
        gain_arrival(d).wait_recv()
    for c in range(chunks):
        for d in range(1, zero):
            part_copy(c, d).wait_send()
            serve_copy(c, d).wait_send()
            serve_arrival(c, d).wait_recv()


def place(counts, width, *refs):
    (fresh, serve, scales, gain, sq, sk, sv, cq, ck, cv, norm, fq, fk, fv, narrow, sem, norm_sem) = refs
    copies = []
    c = 0
    for full, column, own, count in ((sq, cq, fq, counts[0]), (sk, ck, fk, counts[1]), (sv, cv, fv, counts[2])):
        for j in range(count):
            at = pl.ds(j * width, width)
            copies.append(pltpu.make_async_copy(fresh.at[c], own.at[:, at], sem.at[0, c]))
            copies.append(pltpu.make_async_copy(serve.at[c], full.at[:, at], sem.at[1, c]))
            copies.append(pltpu.make_async_copy(scales.at[c], column.at[:, at], sem.at[2, c]))
            c += 1
    for copy in copies:
        copy.start()
    lanes = norm.shape[1]
    narrow[...] = gain[...].reshape(norm.shape[0], lanes).astype(jnp.bfloat16)
    copies.append(pltpu.make_async_copy(narrow, norm, norm_sem))
    copies[-1].start()
    for copy in copies:
        copy.wait()


def solution(mesh):
    zero, tp = mesh.shape["zero"], mesh.shape["tp"]
    group = zero * tp

    def body(w_query, avg_query, w_key, avg_key, w_value, avg_value, norm_train, norm_step):
        rows = w_query.shape[0]
        widths = [w.shape[1] for w in (w_query, w_key, w_value)]
        width = math.gcd(CHUNK, *widths)
        counts = tuple(w // width for w in widths)
        chunks = sum(counts)
        piece = norm_train.shape[0]
        lanes = math.gcd(piece, LANES)
        f32, bf16 = jnp.float32, jnp.bfloat16
        hbm = pl.BlockSpec(memory_space=pl.ANY)
        vmem = pl.BlockSpec(memory_space=pltpu.VMEM)
        dma = pltpu.SemaphoreType.DMA
        staged = 2 * chunks * rows * width * 4
        others = max(zero - 1, 1)
        results = pl.pallas_call(
            functools.partial(exchange, zero, tp, counts, width),
            out_shape=(
                pltpu.VMEM((chunks, rows, width), f32),
                pltpu.VMEM((chunks, zero * rows, width), bf16),
                pltpu.VMEM((chunks, 1, width), f32),
                pltpu.VMEM((group, piece // lanes, lanes), f32),
            ),
            in_specs=[hbm] * 6 + [vmem] * 2,
            out_specs=(vmem,) * 4,
            scratch_shapes=[
                pltpu.VMEM((chunks, rows, width), f32),
                pltpu.VMEM((chunks, rows, width), f32),
                pltpu.VMEM((zero, chunks, 1, width), f32),
                dma((2, chunks)),
                dma((chunks, others)),
                dma((chunks, zero)),
                dma((chunks, others)),
                dma((chunks, zero)),
                dma((max(group - 1, 1),)),
                dma((group,)),
            ],
            compiler_params=pltpu.CompilerParams(
                collective_id=0, has_side_effects=True, vmem_limit_bytes=staged + (4 << 20)
            ),
        )(
            w_query, avg_query, w_key, avg_key, w_value, avg_value,
            norm_train.reshape(-1, lanes), norm_step.reshape(-1, lanes),
        )
        shape = jax.ShapeDtypeStruct
        outs = pl.pallas_call(
            functools.partial(place, counts, width),
            out_shape=(
                *(shape((zero * rows, w), bf16) for w in widths),
                *(shape((1, w), f32) for w in widths),
                shape((group * piece // lanes, lanes), bf16),
                *(shape((rows, w), f32) for w in widths),
            ),
            in_specs=[vmem] * 4,
            out_specs=(hbm,) * 10,
            scratch_shapes=[
                pltpu.VMEM((group * piece // lanes, lanes), bf16),
                dma((3, chunks)),
                dma,
            ],
            compiler_params=pltpu.CompilerParams(vmem_limit_bytes=2 << 20),
        )(*results)
        sq, sk, sv, cq, ck, cv, norm, fq, fk, fv = outs
        return sq, sk, sv, cq.reshape(-1), ck.reshape(-1), cv.reshape(-1), norm.reshape(-1), fq, fk, fv

    weights = P(("job", "zero"), "tp")
    in_specs = (weights,) * 6 + (P(("job", "zero", "tp")),) * 2
    out_specs = (P("job", "tp"),) * 3 + (P(("job", "tp")),) * 3 + (P("job"),) + (weights,) * 3
    return jax.shard_map(body, mesh=mesh, in_specs=in_specs, out_specs=out_specs, check_vma=False)
```

time: 94.7 us -> 26.9 us (0.28)
  Pallas kernels: 0 us -> 24.7 us
  blocking collectives: 23.1 us -> 0 us
  other arithmetic: 22.6 us -> 0 us
  waiting for transfers between devices: 20.6 us -> 0 us
  between operations: 13.9 us -> 0.66 us
  local copies, waits for them, and re-layouts: 14.2 us -> 1.36 us
    pallas_call x0 -> x2, Pallas kernels: none -> 24.7 us  [the longest x1 16.2 us: body(): pl.pallas_call(functools.partial(exchange, zero, tp, counts, width), out_...]
    all_gather x3 -> x0, waiting for transfers between devices: 20.5 us -> none  [the longest x1 20.5 us: body(): lax.all_gather(narrow_query, 'zero', axis=0, tiled=True)]
    all_gather x1 -> x0, blocking collectives: 20.4 us -> none  [body(): lax.all_gather((norm_train + norm_step).astype(jnp.bfloat16), ('zero', 't...]
    unnamed x29 -> x4, local copies, waits for them, and re-layouts: 14.2 us -> 1.36 us
    reduce_sum x2 -> x0, other arithmetic: 12 us -> none  [the longest x1 9.99 us: body(): jnp.sum(fresh_query * fresh_query, axis=0)]
    convert_element_type x4 -> x0, other arithmetic: 10.5 us -> none  [the longest x1 6.67 us: body(): (fresh_query / column_query).astype(jnp.bfloat16)]
    psum x1 -> x0, blocking collectives: 2.63 us -> none  [body(): lax.psum((jnp.sum(fresh_query * fresh_query, axis=0), jnp.sum(fresh_key *...]
  transfers between devices with their start and end apart: 3 -> 0, of which waited for: 1 -> 0; matrix products, arithmetic and copies ran while one was open for 9% -> 0% of each run, Pallas kernels for 0% -> 0%
where the time goes in v1:
time: 26.9 us; the launch traced here: 26.8 us
  Pallas kernels  24.7 us (92%)
  local copies, waits for them, and re-layouts  1.36 us (5%)
  between operations  0.66 us (2%)
    pallas_call x1, Pallas kernels, body(): pl.pallas_call(functools.partial(exchange, zero, tp, counts, width), out_...  16.2 us
    pallas_call x1, Pallas kernels, body(): pl.pallas_call(functools.partial(place, counts, width), out_shape=(*(shap...  8.57 us
    unnamed x4, local copies, waits for them, and re-layouts  1.36 us

profile of v1, /device:TPU:0, one launch (start us, length us, event | category | flops | bytes accessed | tf_op | source)
XLA Modules:
  0.0 26.8 jit_solution(17835789187758833502)
XLA Ops:
  0.6 0.0 copy-start
  0.7 0.7 %copy-done = f32[512]{0:T(512)S(1)} copy-done((f32[512]{0:T(512)S(1)}, f32[512]{0:T(512)}, u32[]{:S(2)}) %copy-start) | copy-done | bytes 2072
  1.3 0.0 copy-start.1
  1.3 0.7 %copy-done.1 = f32[512]{0:T(512)S(1)} copy-done((f32[512]{0:T(512)S(1)}, f32[512]{0:T(512)}, u32[]{:S(2)}) %copy-start.1) | copy-done | bytes 2072
  2.0 16.2 %shard_map.159 = (f32[6,2048,256]{2,1,0:T(8,128)S(1)}, bf16[6,4096,256]{2,1,0:T(8,128)(2,1)S(1)}, f32[6,1,256]{2,1,0:T(1,128)S(1)}, f32[8,4,128]{2,1,0:T(4,128)S(1)}) custom-call(f32[2048,1024]{1,0:T(8,128)} %refs_0_.1, f32[2048,1024]{1,0:T(8,128)} %refs_1_.1, f32[2048,256]{1,0:T(8,128)} %refs_2_.1, f32[2048,256]{1,0:T(8,128)} %refs_3_.1, ...), custom_call_target="tpu_custom_call" | custom-call | tf_op jit(solution)/shard_map/pallas_call | solution.py:206
  18.2 8.6 %shard_map.160 = (bf16[4096,1024]{1,0:T(8,128)(2,1)}, bf16[4096,256]{1,0:T(8,128)(2,1)}, bf16[4096,256]{1,0:T(8,128)(2,1)}, f32[1,1024]{1,0:T(1,128)}, f32[1,256...) custom-call(f32[6,2048,256]{2,1,0:T(8,128)S(1)} %get-tuple-element.2, ...), custom_call_target="tpu_custom_call" | custom-call | tf_op jit(solution)/shard_map/pallas_call | solution.py:236
Async XLA Ops:
  0.6 0.7 %copy-start = (f32[512]{0:T(512)S(1)}, f32[512]{0:T(512)}, u32[]{:S(2)}) copy-start(f32[512]{0:T(512)} %param.14) | copy-start | bytes 6148
  1.3 0.7 %copy-start.1 = (f32[512]{0:T(512)S(1)}, f32[512]{0:T(512)}, u32[]{:S(2)}) copy-start(f32[512]{0:T(512)} %param.15) | copy-start | bytes 6148

commit v2 on v1

--- a/solution.py
+++ b/solution.py
@@ -12,8 +12,9 @@
 LANES = 128
 CHUNK = 256
 AHEAD = 3
+SPLIT = 2
 LAG = 1
-STEP = 64
+STEP = 128
 MESH = pl.DeviceIdType.MESH
 
 
@@ -23,25 +24,40 @@
 
 def exchange(zero, tp, counts, width, *refs):
     (wq, aq, wk, ak, wv, av, train, step, fresh, serve, scales, gain,
-     w_buf, a_buf, parts, read_sem, part_send, part_recv, send, recv, gain_send, gain_recv) = refs
-    chunks = sum(counts)
+     w_buf, a_buf, norm_buf, parts, read_sem, norm_sem, part_send, part_recv, send, recv, gain_send, gain_recv) = refs
     rows = wq.shape[0]
     me = lax.axis_index("zero")
     my_tp = lax.axis_index("tp")
     where = []
     for w, a, count in ((wq, aq, counts[0]), (wk, ak, counts[1]), (wv, av, counts[2])):
         where += [(w, a, j * width) for j in range(count)]
+    cuts = []
+    for c in range(len(where)):
+        parted = SPLIT if c == 0 and width % (SPLIT * LANES) == 0 else 1
+        cuts += [(c, k * (width // parted), width // parted) for k in range(parted)]
+    pieces = len(cuts)
+
+    def cut(c):
+        chunk, sub, wide = cuts[c]
+        return chunk, pl.ds(sub, wide), wide
 
     def reads(c):
-        w, a, at = where[c]
+        chunk, sub, wide = cuts[c]
+        w, a, at = where[chunk]
+        here, there = pl.ds(at + sub, wide), pl.ds(sub, wide)
         return (
-            pltpu.make_async_copy(w.at[:, pl.ds(at, width)], w_buf.at[c], read_sem.at[0, c]),
-            pltpu.make_async_copy(a.at[:, pl.ds(at, width)], a_buf.at[c], read_sem.at[1, c]),
-        )
-
-    for c in range(min(AHEAD, chunks)):
+            pltpu.make_async_copy(w.at[:, here], w_buf.at[chunk, :, there], read_sem.at[0, c]),
+            pltpu.make_async_copy(a.at[:, here], a_buf.at[chunk, :, there], read_sem.at[1, c]),
+        )
+
+    for c in range(min(AHEAD, pieces)):
         for copy in reads(c):
             copy.start()
+    norm_reads = [
+        pltpu.make_async_copy(ref, norm_buf.at[k], norm_sem.at[k]) for k, ref in enumerate((train, step))
+    ]
+    for copy in norm_reads:
+        copy.start()
 
     group = zero * tp
     mine = me * tp + my_tp
@@ -55,11 +71,14 @@
         pl.semaphore_signal(barrier, inc=1, device_id=member(d)[1], device_id_type=MESH)
     pl.semaphore_wait(barrier, group - 1)
 
-    gain[mine] = train[...] + step[...]
+
+    def sums(c, owner):
+        chunk, at, _ = cut(c)
+        return parts.at[owner, chunk, :, at]
 
     def part_copy(c, d):
         return pltpu.make_async_remote_copy(
-            src_ref=parts.at[me, c], dst_ref=parts.at[me, c],
+            src_ref=sums(c, me), dst_ref=sums(c, me),
             send_sem=part_send.at[c, d - 1], recv_sem=part_recv.at[c, me],
             device_id={"zero": lax.rem(me + d, zero)}, device_id_type=MESH,
         )
@@ -67,13 +86,14 @@
     def part_arrival(c, d):
         other = lax.rem(me + d, zero)
         return pltpu.make_async_remote_copy(
-            src_ref=parts.at[other, c], dst_ref=parts.at[other, c],
+            src_ref=sums(c, other), dst_ref=sums(c, other),
             send_sem=part_send.at[c, d - 1], recv_sem=part_recv.at[c, other],
             device_id={"zero": other}, device_id_type=MESH,
         )
 
     def block(c, owner):
-        return serve.at[c, pl.ds(pl.multiple_of(owner * rows, rows), rows), :]
+        chunk, at, _ = cut(c)
+        return serve.at[chunk, pl.ds(pl.multiple_of(owner * rows, rows), rows), at]
 
     def serve_copy(c, d):
         return pltpu.make_async_remote_copy(
@@ -108,47 +128,52 @@
     block_rows = row_step(rows)
 
     def mix(c):
-        if c + AHEAD < chunks:
+        if c + AHEAD < pieces:
             for copy in reads(c + AHEAD):
                 copy.start()
         for copy in reads(c):
             copy.wait()
+        chunk, columns, wide = cut(c)
 
         def one(i, total):
             at = pl.ds(pl.multiple_of(i * block_rows, block_rows), block_rows)
-            new = keep_rate * a_buf[c, at, :] + (1.0 - keep_rate) * w_buf[c, at, :]
-            fresh[c, at, :] = new
-            return total + jnp.sum((new * new).reshape(block_rows // 8, 8, width), axis=0)
-
-        total = lax.fori_loop(0, rows // block_rows, one, jnp.zeros((8, width), jnp.float32))
-        parts[me, c] = jnp.sum(total, axis=0, keepdims=True)
+            new = keep_rate * a_buf[chunk, at, columns] + (1.0 - keep_rate) * w_buf[chunk, at, columns]
+            fresh[chunk, at, columns] = new
+            return total + jnp.sum((new * new).reshape(block_rows // 8, 8, wide), axis=0)
+
+        total = lax.fori_loop(0, rows // block_rows, one, jnp.zeros((8, wide), jnp.float32))
+        parts[me, chunk, :, columns] = jnp.sum(total, axis=0, keepdims=True)
         for d in range(1, zero):
             part_copy(c, d).start()
 
     def scale(c):
         for d in range(1, zero):
             part_arrival(c, d).wait_recv()
-        total = parts[0, c]
+        chunk, columns, wide = cut(c)
+        total = parts[0, chunk, :, columns]
         for k in range(1, zero):
-            total = total + parts[k, c]
+            total = total + parts[k, chunk, :, columns]
         column = jnp.sqrt(total)
-        scales[c] = column
-        inverse = jnp.broadcast_to(1.0 / column, (block_rows, width))
+        scales[chunk, :, columns] = column
+        inverse = jnp.broadcast_to(1.0 / column, (block_rows, wide))
 
         def one(i, carry):
             at = pl.ds(pl.multiple_of(i * block_rows, block_rows), block_rows)
             to = pl.ds(pl.multiple_of(me * rows + i * block_rows, block_rows), block_rows)
-            serve[c, to, :] = (fresh[c, at, :] * inverse).astype(jnp.bfloat16)
+            serve[chunk, to, columns] = (fresh[chunk, at, columns] * inverse).astype(jnp.bfloat16)
             return carry
 
         lax.fori_loop(0, rows // block_rows, one, 0)
         for d in range(1, zero):
             serve_copy(c, d).start()
 
-    for c in range(chunks + LAG):
-        if c < chunks:
+    for c in range(pieces + LAG):
+        if c < pieces:
             mix(c)
         if c == 0:
+            for copy in norm_reads:
+                copy.wait()
+            gain[mine] = norm_buf[0] + norm_buf[1]
             for d in range(1, group):
                 gain_copy(d).start()
         if c >= LAG:
@@ -157,7 +182,7 @@
     for d in range(1, group):
         gain_copy(d).wait_send()
         gain_arrival(d).wait_recv()
-    for c in range(chunks):
+    for c in range(pieces):
         for d in range(1, zero):
             part_copy(c, d).wait_send()
             serve_copy(c, d).wait_send()
@@ -198,7 +223,8 @@
         piece = norm_train.shape[0]
         lanes = math.gcd(piece, LANES)
         f32, bf16 = jnp.float32, jnp.bfloat16
-        hbm = pl.BlockSpec(memory_space=pl.ANY)
+        hbm = pl.BlockSpec(memory_space=pltpu.HBM)
+        hold = lambda x: pltpu.with_memory_space_constraint(x, pltpu.HBM)
         vmem = pl.BlockSpec(memory_space=pltpu.VMEM)
         dma = pltpu.SemaphoreType.DMA
         staged = 2 * chunks * rows * width * 4
@@ -211,17 +237,19 @@
                 pltpu.VMEM((chunks, 1, width), f32),
                 pltpu.VMEM((group, piece // lanes, lanes), f32),
             ),
-            in_specs=[hbm] * 6 + [vmem] * 2,
+            in_specs=[hbm] * 8,
             out_specs=(vmem,) * 4,
             scratch_shapes=[
                 pltpu.VMEM((chunks, rows, width), f32),
                 pltpu.VMEM((chunks, rows, width), f32),
+                pltpu.VMEM((2, piece // lanes, lanes), f32),
                 pltpu.VMEM((zero, chunks, 1, width), f32),
-                dma((2, chunks)),
-                dma((chunks, others)),
-                dma((chunks, zero)),
-                dma((chunks, others)),
-                dma((chunks, zero)),
+                dma((2, chunks + SPLIT)),
+                dma((2,)),
+                dma((chunks + SPLIT, others)),
+                dma((chunks + SPLIT, zero)),
+                dma((chunks + SPLIT, others)),
+                dma((chunks + SPLIT, zero)),
                 dma((max(group - 1, 1),)),
                 dma((group,)),
             ],
@@ -229,8 +257,8 @@
                 collective_id=0, has_side_effects=True, vmem_limit_bytes=staged + (4 << 20)
             ),
         )(
-            w_query, avg_query, w_key, avg_key, w_value, avg_value,
-            norm_train.reshape(-1, lanes), norm_step.reshape(-1, lanes),
+            *map(hold, (w_query, avg_query, w_key, avg_key, w_value, avg_value)),
+            hold(norm_train.reshape(-1, lanes)), hold(norm_step.reshape(-1, lanes)),
         )
         shape = jax.ShapeDtypeStruct
         outs = pl.pallas_call(

time: 26.9 us -> 25.7 us (0.955)
  local copies, waits for them, and re-layouts: 1.36 us -> 0 us
    unnamed x4 -> x0, local copies, waits for them, and re-layouts: 1.36 us -> none
where the time goes in v2:
time: 25.7 us; the launch traced here: 25.6 us
  Pallas kernels  24.9 us (97%)
  between operations  0.65 us (3%)
    pallas_call x1, Pallas kernels, body(): pl.pallas_call(functools.partial(exchange, zero, tp, counts, width), out_...  16.4 us
    pallas_call x1, Pallas kernels, body(): pl.pallas_call(functools.partial(place, counts, width), out_shape=(*(shap...  8.57 us

profile of v2, /device:TPU:0, one launch (start us, length us, event | category | flops | bytes accessed | tf_op | source)
XLA Modules:
  0.0 25.6 jit_solution(4831377306105476256)
XLA Ops:
  0.6 16.4 %shard_map.159 = (f32[6,2048,256]{2,1,0:T(8,128)S(1)}, bf16[6,4096,256]{2,1,0:T(8,128)(2,1)S(1)}, f32[6,1,256]{2,1,0:T(1,128)S(1)}, f32[8,4,128]{2,1,0:T(4,128)S(1)}) custom-call(f32[2048,1024]{1,0:T(8,128)} %refs_0_.1, f32[2048,1024]{1,0:T(8,128)} %refs_1_.1, f32[2048,256]{1,0:T(8,128)} %refs_2_.1, f32[2048,256]{1,0:T(8,128)} %refs_3_.1, ...), custom_call_target="tpu_custom_call" | custom-call | tf_op jit(solution)/shard_map/pallas_call | solution.py:232
  17.0 8.6 %shard_map.160 = (bf16[4096,1024]{1,0:T(8,128)(2,1)}, bf16[4096,256]{1,0:T(8,128)(2,1)}, bf16[4096,256]{1,0:T(8,128)(2,1)}, f32[1,1024]{1,0:T(1,128)}, f32[1,256...) custom-call(f32[6,2048,256]{2,1,0:T(8,128)S(1)} %get-tuple-element.2, ...), custom_call_target="tpu_custom_call" | custom-call | tf_op jit(solution)/shard_map/pallas_call | solution.py:264
